TPU v7x, 1024 devices: a whole 8x8x8 slice. The times are simulated.
1024 devices in a mesh: mem: 64 (over x_hi, y, core), patch: 16 (over x_lo, z).
Axes of the slice: x: 8 (x_hi: 4, x_lo: 2; x = x_hi * 2 + x_lo), y: 8, z: 8, core: 2. Of those that a mesh axis runs over, the one named last changes fastest.
Arguments:
- ens: bfloat16 [2, 256, 8, 131072], P(None, 'mem', None, 'patch'), may hold values from -6 to 6
- obs_pert: bfloat16 [2, 256, 8192], P(None, None, 'patch'), may hold values from -6 to 6
- obs_innov: bfloat16 [2, 8192], P(None, 'patch'), may hold values from -6 to 6
- obs_pos: bfloat16 [2, 8192], P(None, 'patch'), may hold values from 0 to 1
- obs_prec: bfloat16 [2, 8192], P(None, 'patch'), may hold values from 0.25 to 4
Outputs:
- analysed: bfloat16 [2, 256, 8, 131072], P(None, 'mem', None, 'patch')
All inputs are finite; a program needn't handle non-finite values.
Results may differ from a plain program's by a relative error of at most 0.0058.
Values may be sent and summed in bfloat16 or wider, within the bound.
No kernel may reach another device: no remote copies, remote signals or barrier semaphores. Data moves between devices by JAX's collectives and lax.ppermute only.
A program may use at most 64 MiB of HBM per device.

v0:
```python
import jax
import jax.numpy as jnp
from jax import lax
from jax.sharding import Mesh
from jax.sharding import PartitionSpec as P

NS_ITERS = 2
MEM = ("mem_0", "mem_1", "mem_2")


loc_scale = 0.5


def extended(block, sides, width):
    for axis, dim in sides:
        count = lax.axis_size(axis)
        forward = [(i, i + 1) for i in range(count - 1)]
        forward.append((count - 1, 0))
        backward = [(target, source) for source, target in forward]
        low = lax.ppermute(
            lax.slice_in_dim(block, block.shape[dim] - width, None, axis=dim), axis, forward
        )
        high = lax.ppermute(lax.slice_in_dim(block, 0, width, axis=dim), axis, backward)
        block = jnp.concatenate([low, block, high], axis=dim)
    return block


def cut_along(value, dim, length):
    before, after = (value.shape[:dim], value.shape[dim + 1 :])
    return jnp.moveaxis(value.reshape(*before, length, -1, *after), dim, 0)


def joined_along(pieces, dim):
    dims = list(pieces.shape[1:])
    dims[dim] *= pieces.shape[0]
    return jnp.moveaxis(pieces, 0, dim).reshape(dims)


def moved_by_axis(pieces, axes, order):
    inside = pieces.shape[1:]
    filled = pieces.reshape(*(lax.axis_size(a) for a in axes), *inside)
    for k in order:
        filled = lax.all_to_all(filled, axes[k], k, k, tiled=True)
    return filled.reshape(-1, *inside)


def two_step_exchange(value, groups, order, split_dim, concat_dim):
    length = lax.axis_size(groups[0]) * lax.axis_size(groups[1])
    pieces = cut_along(value, split_dim, length)
    return joined_along(moved_by_axis(pieces, groups, order), concat_dim)


def matmul(left, right):
    return jnp.einsum("sij,sjk->sik", left, right, precision=lax.Precision.HIGHEST)


def local_terms(deviations, innovation, position, precision, offset, center):
    distance = position.astype(jnp.float32) + offset - center
    taper = jnp.exp(-0.5 * (distance / loc_scale) ** 2)
    obs_weight = taper * precision.astype(jnp.float32)
    scaled = (deviations.astype(jnp.float32) * obs_weight[:, None, :]).astype(jnp.bfloat16)
    gram_sum = jnp.einsum("skn,sjn->skj", scaled, deviations, preferred_element_type=jnp.float32)
    innov_sum = jnp.einsum("skn,sn->sk", scaled, innovation, preferred_element_type=jnp.float32)
    return (gram_sum, innov_sum)


def transform_weights(gram_sum, innov_sum, members):
    identity = jnp.eye(members, dtype=jnp.float32)[None]
    system = (members - 1.0) * identity + gram_sum
    frobenius = jnp.sqrt(jnp.sum(system * system, axis=(1, 2)))[:, None, None]
    current = system / frobenius
    inverse = jnp.broadcast_to(identity, system.shape)
    for sweep in range(NS_ITERS):
        factor = 1.5 * identity - 0.5 * matmul(inverse, current)
        if sweep + 1 < NS_ITERS:
            current = matmul(current, factor)
        inverse = matmul(factor, inverse)
    inner = jnp.einsum("sjk,sk->sj", inverse, innov_sum, precision=lax.Precision.HIGHEST)
    mean_weight = (
        jnp.einsum("sjk,sk->sj", inverse, inner, precision=lax.Precision.HIGHEST)
        / frobenius[:, :, 0]
    )
    spread = inverse * jnp.sqrt((members - 1.0) / frobenius)
    return (spread + mean_weight[:, :, None]).astype(jnp.bfloat16)


def analyse(block, weights):
    average = jnp.mean(block.astype(jnp.float32), axis=1, keepdims=True)
    anomaly = (block.astype(jnp.float32) - average).astype(jnp.bfloat16)
    mixed = jnp.einsum("sjlg,sjk->sklg", anomaly, weights, preferred_element_type=jnp.float32)
    return (average + mixed).astype(jnp.bfloat16)


def on_device(ens, obs_pert, obs_innov, obs_pos, obs_prec):
    members = obs_pert.shape[1]
    width = obs_pert.shape[2]
    center = (lax.axis_index(MEM).astype(jnp.float32) + 0.5) / lax.axis_size(MEM)
    stacked = jnp.concatenate(
        [obs_pert, obs_innov[:, None, :], obs_pos[:, None, :], obs_prec[:, None, :]], axis=1
    )
    padded = extended(stacked, (("patch", 2),), width)
    offsets = jnp.repeat(jnp.array([-1.0, 0.0, 1.0], jnp.float32), width)
    gram_sum, innov_sum = local_terms(
        padded[:, :members],
        padded[:, members],
        padded[:, members + 1],
        padded[:, members + 2],
        offsets,
        center,
    )
    weights = transform_weights(gram_sum, innov_sum, members)
    gathered = two_step_exchange(ens, (("mem_0", "mem_1"), "mem_2"), (1, 0), 3, 1)
    return lax.all_to_all(analyse(gathered, weights), MEM, split_axis=1, concat_axis=3, tiled=True)


def solution(mesh):
    torus = Mesh(
        mesh.devices.reshape(4, 8, 2, mesh.shape["patch"]), ("mem_0", "mem_1", "mem_2", "patch")
    )
    return jax.shard_map(
        on_device,
        mesh=torus,
        in_specs=(
            P(None, MEM, None, "patch"),
            P(None, None, "patch"),
            P(None, "patch"),
            P(None, "patch"),
            P(None, "patch"),
        ),
        out_specs=P(None, MEM, None, "patch"),
        check_vma=False,
    )
```

profile of v0, /device:TPU:39, one launch (start us, length us, event | category | flops | bytes accessed | tf_op | source)
XLA Modules:
  0.0 131.1 jit_solution(310018754216956011)
XLA Ops:
  0.0 0.0 copy-start.1
  0.0 0.8 copy.45
  0.8 0.7 copy.46
  1.5 0.7 copy.47
  2.1 1.1 pad_maximum_fusion.1
  3.2 0.4 copy.48
  3.7 4.9 %collective-permute-start = (bf16[2,259,512]{2,0,1:T(2,128)(2,1)S(1)}, bf16[2,259,512]{2,0,1:T(2,128)(2,1)S(1)}, u32[]{:S(2)}, u32[]{:S(2)}) collective-permute-start(bf16[2,259,512]{2,0,1:T(2,128)(2,1)S(1)} %copy.48), channel_id=1, source_target_pairs={{0,1},{1,2},{2,3},{3,4},{4,5},{5,6},{6,7},{7,8},{8,9},{9,10},{10,1... | collective-permute-start | bytes 1591304 | tf_op jit(solution)/shard_map/ppermute | solution.py:20
  8.6 14.0 %collective-permute-start.1 = (bf16[2,259,512]{2,0,1:T(2,128)(2,1)S(1)}, bf16[2,259,512]{2,0,1:T(2,128)(2,1)S(1)}, u32[]{:S(2)}, u32[]{:S(2)}) collective-permute-start(bf16[2,259,512]{2,0,1:T(2,128)(2,1)S(1)} %copy.48), channel_id=1, source_target_pairs={{1,0},{2,1},{3,2},{4,3},{5,4},{6,5},{7,6},{8,7},{9,8},{10,9},{11,1... | collective-permute-start | bytes 1591304 | tf_op jit(solution)/shard_map/ppermute | solution.py:23
  22.6 0.0 copy-done.1
  22.6 0.3 copy.68
  22.9 0.9 copy.42
  23.7 5.2 %all_to_all.28 = bf16[32,2,2,4,8,128]{5,3,0,4,2,1:T(4,128)(2,1)S(1)} all-to-all(bf16[32,2,2,4,8,128]{5,3,0,4,2,1:T(4,128)(2,1)S(1)} %copy.42), channel_id=1, replica_groups=mesh['mem_0'=4,'mem_1'=8,'mem_2'=2,'patch'=16] {'mem_2'}, dimensions={1} | all-to-all | bytes 2097152 | tf_op jit(solution)/shard_map/all_to_all | solution.py:43
  28.9 0.0 copy-start.2
  28.9 1.6 %copy.43 = bf16[32,2,2,4,8,128]{5,3,1,4,2,0:T(4,128)(2,1)} copy(bf16[32,2,2,4,8,128]{5,3,0,4,2,1:T(4,128)(2,1)S(1)} %all_to_all.28) | data formatting | bytes 2097152 | tf_op jit(solution)/shard_map/all_to_all | solution.py:43
  30.5 0.0 copy-start
  30.5 12.3 %all-to-all-start.1 = ((bf16[32,2,2,4,8,128]{5,3,1,4,2,0:T(4,128)(2,1)}), bf16[32,2,2,4,8,128]{5,3,1,4,2,0:T(4,128)(2,1)S(1)}, u32[]{:S(2)}, u32[]{:S(2)}) async-start(bf16[32,2,2,4,8,128]{5,3,1,4,2,0:T(4,128)(2,1)} %copy.43), calls=%async_computation.1 | async-start | bytes 2097152 | tf_op jit(solution)/shard_map/all_to_all | solution.py:43
  42.7 0.0 copy-done.2
  42.7 0.1 broadcast_in_dim.28
  42.9 0.0 collective-permute-done
  42.9 0.1 copy.50
  43.0 0.0 collective-permute-done.1
  43.0 0.1 copy.51
  43.0 0.0 copy-done
  43.1 0.1 pad_maximum_fusion
  43.2 0.1 fusion.34
  43.3 0.5 fusion
  43.8 0.7 multiply_reduce_fusion
  44.5 0.7 fusion.7
  45.3 0.6 fusion.17
  45.9 0.7 fusion.23
  46.6 0.7 fusion.6
  47.3 0.7 fusion.42
  47.9 0.5 fusion.39
  48.5 0.6 fusion.37
  49.0 0.1 bitcast_divide_fusion
  49.1 25.0 %all-to-all-done.1 = bf16[32,2,2,4,8,128]{5,3,1,4,2,0:T(4,128)(2,1)S(1)} async-done(((bf16[32,2,2,4,8,128]{5,3,1,4,2,0:T(4,128)(2,1)}), bf16[32,2,2,4,8,128]{5,3,1,4,2,0:T(4,128)(2,1)S(1)}, u32[]{:S(2)}, u32[]{:S(2)}) %all-to-all-start.1) | async-done | bytes 1048608 | tf_op jit(solution)/shard_map/all_to_all | solution.py:43
  74.1 0.3 copy_convert_fusion
  74.4 0.5 copy.52
  75.0 0.3 fusion.12
  75.2 0.6 add_convert_fusion
  75.8 0.7 copy.54
  76.5 53.5 %all_to_all.29 = bf16[2,256,8,128]{3,2,0,1:T(8,128)(2,1)S(1)} all-to-all(bf16[2,256,8,128]{3,2,0,1:T(8,128)(2,1)S(1)} %copy.54), channel_id=1, replica_groups=mesh['mem_0'=4,'mem_1'=8,'mem_2'=2,'patch'=16] {'mem_0','mem_1','mem_2'}, dimensions={1} | all-to-all | bytes 2097152 | tf_op jit(solution)/shard_map/all_to_all | solution.py:113
  130.0 1.2 copy.81
  (9 shorter events, 0.1 us)
Async XLA Ops:
  0.0 22.6 %copy-start.1 = (bf16[2,4,8,8192]{3,2,1,0:T(8,128)(2,1)S(1)}, bf16[2,4,8,8192]{3,2,1,0:T(8,128)(2,1)}, u32[]{:S(2)}) copy-start(bf16[2,4,8,8192]{3,2,1,0:T(8,128)(2,1)} %param.6) | copy-start | bytes 3145732
  3.7 39.2 %collective-permute-start = (bf16[2,259,512]{2,0,1:T(2,128)(2,1)S(1)}, bf16[2,259,512]{2,0,1:T(2,128)(2,1)S(1)}, u32[]{:S(2)}, u32[]{:S(2)}) collective-permute-start(bf16[2,259,512]{2,0,1:T(2,128)(2,1)S(1)} %copy.48), channel_id=1, source_target_pairs={{0,1},{1,2},{2,3},{3,4},{4,5},{5,6},{6,7},{7,8},{8,9},{9,10},{10,1... | collective-permute-start | bytes 1591304 | tf_op jit(solution)/shard_map/ppermute | solution.py:20
  8.6 34.4 %collective-permute-start.1 = (bf16[2,259,512]{2,0,1:T(2,128)(2,1)S(1)}, bf16[2,259,512]{2,0,1:T(2,128)(2,1)S(1)}, u32[]{:S(2)}, u32[]{:S(2)}) collective-permute-start(bf16[2,259,512]{2,0,1:T(2,128)(2,1)S(1)} %copy.48), channel_id=1, source_target_pairs={{1,0},{2,1},{3,2},{4,3},{5,4},{6,5},{7,6},{8,7},{9,8},{10,9},{11,1... | collective-permute-start | bytes 1591304 | tf_op jit(solution)/shard_map/ppermute | solution.py:23
  28.9 13.8 %copy-start.2 = (f32[3]{0:T(128)S(1)}, f32[3]{0:T(128)}, u32[]{:S(2)}) copy-start(f32[3]{0:T(128)} %constant.47.clone) | copy-start | bytes 40
  30.5 12.6 %copy-start = (bf16[2,256,512]{2,1,0:T(8,128)(2,1)S(1)}, bf16[2,256,512]{2,1,0:T(8,128)(2,1)}, u32[]{:S(2)}) copy-start(bf16[2,256,512]{2,1,0:T(8,128)(2,1)} %param.7) | copy-start | bytes 1572868
  30.5 43.6 %all-to-all-start.1 = ((bf16[32,2,2,4,8,128]{5,3,1,4,2,0:T(4,128)(2,1)}), bf16[32,2,2,4,8,128]{5,3,1,4,2,0:T(4,128)(2,1)S(1)}, u32[]{:S(2)}, u32[]{:S(2)}) async-start(bf16[32,2,2,4,8,128]{5,3,1,4,2,0:T(4,128)(2,1)} %copy.43), calls=%async_computation.1 | async-start | bytes 2097152 | tf_op jit(solution)/shard_map/all_to_all | solution.py:43
where the time goes:
time: 132 us; the launch traced here: 131 us
  blocking collectives  58.6 us (44%)
  starting transfers between devices  31.2 us (24%)
  waiting for transfers between devices  25 us (19%)
  local copies, waits for them, and re-layouts  7.83 us (6%)
  matrix products  6.26 us (5%)
  other arithmetic  2.02 us (2%)
    all_to_all x1, blocking collectives, on_device(): lax.all_to_all(analyse(gathered, weights), MEM, split_axis=1, concat_axis...  53.5 us
    all_to_all x1, waiting for transfers between devices, moved_by_axis(): filled = lax.all_to_all(filled, axes[k], k, k, tiled=True)  25 us
    ppermute x1, starting transfers between devices, extended(): lax.ppermute(lax.slice_in_dim(block, 0, width, axis=dim), axis, backward)  14 us
    all_to_all x1, starting transfers between devices, moved_by_axis(): filled = lax.all_to_all(filled, axes[k], k, k, tiled=True)  12.3 us
    all_to_all x1, blocking collectives, moved_by_axis(): filled = lax.all_to_all(filled, axes[k], k, k, tiled=True)  5.16 us
    ppermute x1, starting transfers between devices, extended(): lax.ppermute(lax.slice_in_dim(block, block.shape[dim] - width, None, axis...  4.91 us
    dot_general x5, matrix products, matmul(): jnp.einsum('sij,sjk->sik', left, right, precision=lax.Precision.HIGHEST)  3.35 us
  transfers between devices with their start and end apart: 3, of which 1 were waited for; matrix products, arithmetic and copies ran while one was open for 7% of the time, Pallas kernels for 0%

commit v1 on v0

v1 whole, which is shorter than its diff:
```python
import jax
import jax.numpy as jnp
from jax import lax
from jax.sharding import PartitionSpec as P


NS_ITERS = 2
MEM = "mem"
LOC_SCALE = 0.5


def halo(block):
    count = lax.axis_size("patch")
    forward = [(i, (i + 1) % count) for i in range(count)]
    backward = [(target, source) for source, target in forward]
    low = lax.ppermute(block, "patch", forward)
    high = lax.ppermute(block, "patch", backward)
    return low, high


def matmul(left, right):
    return jnp.einsum("sij,sjk->sik", left, right, precision=lax.Precision.HIGHEST)


def local_terms(deviations, innovation, position, precision, offset, center):
    distance = position.astype(jnp.float32) + offset - center
    taper = jnp.exp(-0.5 * (distance / LOC_SCALE) ** 2)
    obs_weight = taper * precision.astype(jnp.float32)
    scaled = (deviations.astype(jnp.float32) * obs_weight[:, None, :]).astype(jnp.bfloat16)
    gram_sum = jnp.einsum("skn,sjn->skj", scaled, deviations, preferred_element_type=jnp.float32)
    innov_sum = jnp.einsum("skn,sn->sk", scaled, innovation, preferred_element_type=jnp.float32)
    return gram_sum, innov_sum


def transform_weights(gram_sum, innov_sum, members):
    identity = jnp.eye(members, dtype=jnp.float32)[None]
    system = (members - 1.0) * identity + gram_sum
    frobenius = jnp.sqrt(jnp.sum(system * system, axis=(1, 2)))[:, None, None]
    current = system / frobenius
    inverse = jnp.broadcast_to(identity, system.shape)
    for sweep in range(NS_ITERS):
        factor = 1.5 * identity - 0.5 * matmul(inverse, current)
        if sweep + 1 < NS_ITERS:
            current = matmul(current, factor)
        inverse = matmul(factor, inverse)
    inner = jnp.einsum("sjk,sk->sj", inverse, innov_sum, precision=lax.Precision.HIGHEST)
    mean_weight = (
        jnp.einsum("sjk,sk->sj", inverse, inner, precision=lax.Precision.HIGHEST)
        / frobenius[:, :, 0]
    )
    spread = inverse * jnp.sqrt((members - 1.0) / frobenius)
    return (spread + mean_weight[:, :, None]).astype(jnp.bfloat16)


def analyse(block, weights):
    average = jnp.mean(block.astype(jnp.float32), axis=1, keepdims=True)
    anomaly = (block.astype(jnp.float32) - average).astype(jnp.bfloat16)
    mixed = jnp.einsum("sjlg,sjk->sklg", anomaly, weights, preferred_element_type=jnp.float32)
    return (average + mixed).astype(jnp.bfloat16)


def on_device(ens, obs_pert, obs_innov, obs_pos, obs_prec):
    slabs, own, levels, _ = ens.shape
    members = obs_pert.shape[1]
    ranks = lax.axis_size(MEM)
    pieces = jnp.moveaxis(ens.reshape(slabs, own, levels, ranks, -1), 3, 0)
    gathered = lax.all_to_all(pieces, MEM, 0, 0, tiled=True)
    center = (lax.axis_index(MEM).astype(jnp.float32) + 0.5) / ranks
    stacked = jnp.concatenate(
        [obs_pert, obs_innov[:, None, :], obs_pos[:, None, :], obs_prec[:, None, :]], axis=1
    )
    low, high = halo(stacked)
    padded = jnp.concatenate([low, stacked, high], axis=2)
    offsets = jnp.repeat(jnp.array([-1.0, 0.0, 1.0], jnp.float32), obs_pert.shape[2])
    gram_sum, innov_sum = local_terms(
        padded[:, :members],
        padded[:, members],
        padded[:, members + 1],
        padded[:, members + 2],
        offsets,
        center,
    )
    weights = transform_weights(gram_sum, innov_sum, members)
    block = jnp.moveaxis(gathered, 0, 1).reshape(slabs, members, levels, -1)
    analysed = analyse(block, weights)
    return lax.all_to_all(analysed, MEM, split_axis=1, concat_axis=3, tiled=True)


def solution(mesh):
    return jax.shard_map(
        on_device,
        mesh=mesh,
        in_specs=(
            P(None, MEM, None, "patch"),
            P(None, None, "patch"),
            P(None, "patch"),
            P(None, "patch"),
            P(None, "patch"),
        ),
        out_specs=P(None, MEM, None, "patch"),
        check_vma=False,
    )
```

time: 132 us -> 130 us (0.985)
  the two profiles are of different devices: /device:TPU:39 before, /device:TPU:19 now
where the time goes in v1:
time: 130 us
  blocking collectives  42.6 us (33%)
  waiting for transfers between devices  37.9 us (29%)
  starting transfers between devices  33 us (25%)
  local copies, waits for them, and re-layouts  7.43 us (6%)
  matrix products  6.26 us (5%)
  other arithmetic  2.49 us (2%)
    all_to_all x1, blocking collectives, on_device(): lax.all_to_all(analysed, MEM, split_axis=1, concat_axis=3, tiled=True)  42.6 us
    all_to_all x1, waiting for transfers between devices, on_device(): gathered = lax.all_to_all(pieces, MEM, 0, 0, tiled=True)  37.8 us
    all_to_all x1, starting transfers between devices, on_device(): gathered = lax.all_to_all(pieces, MEM, 0, 0, tiled=True)  14.1 us
    ppermute x1, starting transfers between devices, halo(): high = lax.ppermute(block, 'patch', backward)  14 us
    ppermute x1, starting transfers between devices, halo(): low = lax.ppermute(block, 'patch', forward)  4.91 us
    dot_general x5, matrix products, matmul(): jnp.einsum('sij,sjk->sik', left, right, precision=lax.Precision.HIGHEST)  3.35 us
  transfers between devices with their start and end apart: 3, of which 1 were waited for; matrix products, arithmetic and copies ran while one was open for 7% of the time, Pallas kernels for 0%

profile of v1, /device:TPU:19, one launch (start us, length us, event | category | flops | bytes accessed | tf_op | source)
XLA Modules:
  0.0 129.8 jit_solution(17612855293003805606)
XLA Ops:
  0.0 0.0 copy-start.1
  0.0 0.8 copy.28
  0.8 0.7 copy.29
  1.5 0.7 copy.30
  2.1 1.1 pad_maximum_fusion.1
  3.2 0.4 copy.31
  3.7 4.9 %collective-permute-start = (bf16[2,259,512]{2,0,1:T(2,128)(2,1)S(1)}, bf16[2,259,512]{2,0,1:T(2,128)(2,1)S(1)}, u32[]{:S(2)}, u32[]{:S(2)}) collective-permute-start(bf16[2,259,512]{2,0,1:T(2,128)(2,1)S(1)} %copy.31), channel_id=1, source_target_pairs={{0,1},{1,2},{2,3},{3,4},{4,5},{5,6},{6,7},{7,8},{8,9},{9,10},{10,1... | collective-permute-start | bytes 1591304 | tf_op jit(solution)/shard_map/ppermute | solution.py:16
  8.6 14.0 %collective-permute-start.1 = (bf16[2,259,512]{2,0,1:T(2,128)(2,1)S(1)}, bf16[2,259,512]{2,0,1:T(2,128)(2,1)S(1)}, u32[]{:S(2)}, u32[]{:S(2)}) collective-permute-start(bf16[2,259,512]{2,0,1:T(2,128)(2,1)S(1)} %copy.31), channel_id=1, source_target_pairs={{1,0},{2,1},{3,2},{4,3},{5,4},{6,5},{7,6},{8,7},{9,8},{10,9},{11,1... | collective-permute-start | bytes 1591304 | tf_op jit(solution)/shard_map/ppermute | solution.py:17
  22.6 0.0 copy-done.1
  22.6 0.0 copy-start.2
  22.6 2.3 %copy.27 = bf16[64,2,4,8,128]{4,2,3,1,0:T(4,128)(2,1)} copy(bf16[64,2,4,8,128]{4,3,0,2,1:T(8,128)(2,1)S(1)} %bitcast.52) | data formatting | bytes 2097152 | tf_op jit(solution)/shard_map/transpose | solution.py:66
  24.9 0.0 copy-start
  24.9 14.1 %all-to-all-start = ((bf16[64,2,4,8,128]{4,2,3,1,0:T(4,128)(2,1)}), bf16[64,2,4,8,128]{4,2,3,1,0:T(4,128)(2,1)S(1)}, u32[]{:S(2)}, u32[]{:S(2)}) async-start(bf16[64,2,4,8,128]{4,2,3,1,0:T(4,128)(2,1)} %copy.27), calls=%async_computation | async-start | bytes 2097152 | tf_op jit(solution)/shard_map/all_to_all | solution.py:67
  39.0 0.0 copy-done.2
  39.0 0.1 broadcast_in_dim.28
  39.2 0.0 collective-permute-done
  39.2 0.1 copy.33
  39.3 0.0 collective-permute-done.1
  39.3 0.1 copy.34
  39.3 0.0 copy-done
  39.3 0.1 pad_maximum_fusion
  39.5 0.1 fusion.33
  39.6 0.5 fusion
  40.1 0.7 multiply_reduce_fusion
  40.8 0.7 fusion.7
  41.6 0.6 fusion.16
  42.2 0.7 fusion.22
  42.9 0.7 fusion.6
  43.6 0.7 fusion.41
  44.2 0.5 fusion.38
  44.8 0.6 fusion.36
  45.3 0.1 bitcast_divide_fusion
  45.4 37.8 %all-to-all-done = bf16[64,2,4,8,128]{4,2,3,1,0:T(4,128)(2,1)S(1)} async-done(((bf16[64,2,4,8,128]{4,2,3,1,0:T(4,128)(2,1)}), bf16[64,2,4,8,128]{4,2,3,1,0:T(4,128)(2,1)S(1)}, u32[]{:S(2)}, u32[]{:S(2)}) %all-to-all-start) | async-done | bytes 1048608 | tf_op jit(solution)/shard_map/all_to_all | solution.py:67
  83.2 0.6 convert_bitcast_fusion
  83.9 0.5 copy.35
  84.4 0.4 convert_reduce_fusion
  84.8 0.6 add_convert_fusion
  85.4 0.7 copy.37
  86.1 42.6 %all_to_all.23 = bf16[2,256,8,128]{3,2,0,1:T(8,128)(2,1)S(1)} all-to-all(bf16[2,256,8,128]{3,2,0,1:T(8,128)(2,1)S(1)} %copy.37), channel_id=1, replica_groups=mesh['mem'=64,'patch'=16] {'mem'}, dimensions={1} | all-to-all | bytes 2097152 | tf_op jit(solution)/shard_map/all_to_all | solution.py:86
  128.6 1.2 copy.60
  (9 shorter events, 0.1 us)
Async XLA Ops:
  0.0 22.6 %copy-start.1 = (bf16[2,4,8,8192]{3,2,1,0:T(8,128)(2,1)S(1)}, bf16[2,4,8,8192]{3,2,1,0:T(8,128)(2,1)}, u32[]{:S(2)}) copy-start(bf16[2,4,8,8192]{3,2,1,0:T(8,128)(2,1)} %param.6) | copy-start | bytes 3145732
  3.7 35.5 %collective-permute-start = (bf16[2,259,512]{2,0,1:T(2,128)(2,1)S(1)}, bf16[2,259,512]{2,0,1:T(2,128)(2,1)S(1)}, u32[]{:S(2)}, u32[]{:S(2)}) collective-permute-start(bf16[2,259,512]{2,0,1:T(2,128)(2,1)S(1)} %copy.31), channel_id=1, source_target_pairs={{0,1},{1,2},{2,3},{3,4},{4,5},{5,6},{6,7},{7,8},{8,9},{9,10},{10,1... | collective-permute-start | bytes 1591304 | tf_op jit(solution)/shard_map/ppermute | solution.py:16
  8.6 30.7 %collective-permute-start.1 = (bf16[2,259,512]{2,0,1:T(2,128)(2,1)S(1)}, bf16[2,259,512]{2,0,1:T(2,128)(2,1)S(1)}, u32[]{:S(2)}, u32[]{:S(2)}) collective-permute-start(bf16[2,259,512]{2,0,1:T(2,128)(2,1)S(1)} %copy.31), channel_id=1, source_target_pairs={{1,0},{2,1},{3,2},{4,3},{5,4},{6,5},{7,6},{8,7},{9,8},{10,9},{11,1... | collective-permute-start | bytes 1591304 | tf_op jit(solution)/shard_map/ppermute | solution.py:17
  22.6 16.4 %copy-start.2 = (f32[3]{0:T(128)S(1)}, f32[3]{0:T(128)}, u32[]{:S(2)}) copy-start(f32[3]{0:T(128)} %constant.31.clone) | copy-start | bytes 40
  24.9 14.4 %copy-start = (bf16[2,256,512]{2,1,0:T(8,128)(2,1)S(1)}, bf16[2,256,512]{2,1,0:T(8,128)(2,1)}, u32[]{:S(2)}) copy-start(bf16[2,256,512]{2,1,0:T(8,128)(2,1)} %param.7) | copy-start | bytes 1572868
  24.9 58.3 %all-to-all-start = ((bf16[64,2,4,8,128]{4,2,3,1,0:T(4,128)(2,1)}), bf16[64,2,4,8,128]{4,2,3,1,0:T(4,128)(2,1)S(1)}, u32[]{:S(2)}, u32[]{:S(2)}) async-start(bf16[64,2,4,8,128]{4,2,3,1,0:T(4,128)(2,1)} %copy.27), calls=%async_computation | async-start | bytes 2097152 | tf_op jit(solution)/shard_map/all_to_all | solution.py:67

commit v2 on v1

--- a/solution.py
+++ b/solution.py
@@ -1,6 +1,7 @@
 import jax
 import jax.numpy as jnp
 from jax import lax
+from jax.experimental.layout import Layout, with_layout_constraint
 from jax.sharding import PartitionSpec as P
 
 
@@ -9,12 +10,12 @@
 LOC_SCALE = 0.5
 
 
-def halo(block):
+def from_neighbours(to_next, to_previous):
     count = lax.axis_size("patch")
     forward = [(i, (i + 1) % count) for i in range(count)]
     backward = [(target, source) for source, target in forward]
-    low = lax.ppermute(block, "patch", forward)
-    high = lax.ppermute(block, "patch", backward)
+    low = lax.ppermute(to_next, "patch", forward)
+    high = lax.ppermute(to_previous, "patch", backward)
     return low, high
 
 
@@ -32,16 +33,27 @@
     return gram_sum, innov_sum
 
 
+def packed(gram_sum, innov_sum):
+    high = lax.reduce_precision(innov_sum, 8, 7)
+    rows = jnp.stack([high, innov_sum - high], axis=1).astype(jnp.bfloat16)
+    rows = jnp.pad(rows, ((0, 0), (0, 6), (0, 0)))
+    return jnp.concatenate([gram_sum.astype(jnp.bfloat16), rows], axis=1)
+
+
+def unpacked(message, members):
+    gram_sum = message[:, :members].astype(jnp.float32)
+    return gram_sum, jnp.sum(message[:, members : members + 2].astype(jnp.float32), axis=1)
+
+
 def transform_weights(gram_sum, innov_sum, members):
     identity = jnp.eye(members, dtype=jnp.float32)[None]
     system = (members - 1.0) * identity + gram_sum
     frobenius = jnp.sqrt(jnp.sum(system * system, axis=(1, 2)))[:, None, None]
     current = system / frobenius
-    inverse = jnp.broadcast_to(identity, system.shape)
-    for sweep in range(NS_ITERS):
+    inverse = 1.5 * identity - 0.5 * current
+    for sweep in range(1, NS_ITERS):
+        current = matmul(current, inverse if sweep == 1 else factor)
         factor = 1.5 * identity - 0.5 * matmul(inverse, current)
-        if sweep + 1 < NS_ITERS:
-            current = matmul(current, factor)
         inverse = matmul(factor, inverse)
     inner = jnp.einsum("sjk,sk->sj", inverse, innov_sum, precision=lax.Precision.HIGHEST)
     mean_weight = (
@@ -64,22 +76,15 @@
     members = obs_pert.shape[1]
     ranks = lax.axis_size(MEM)
     pieces = jnp.moveaxis(ens.reshape(slabs, own, levels, ranks, -1), 3, 0)
+    pieces = with_layout_constraint(pieces, Layout((0, 1, 2, 3, 4)))
     gathered = lax.all_to_all(pieces, MEM, 0, 0, tiled=True)
     center = (lax.axis_index(MEM).astype(jnp.float32) + 0.5) / ranks
-    stacked = jnp.concatenate(
-        [obs_pert, obs_innov[:, None, :], obs_pos[:, None, :], obs_prec[:, None, :]], axis=1
+    here, to_next, to_previous = (
+        local_terms(obs_pert, obs_innov, obs_pos, obs_prec, offset, center)
+        for offset in (0.0, -1.0, 1.0)
     )
-    low, high = halo(stacked)
-    padded = jnp.concatenate([low, stacked, high], axis=2)
-    offsets = jnp.repeat(jnp.array([-1.0, 0.0, 1.0], jnp.float32), obs_pert.shape[2])
-    gram_sum, innov_sum = local_terms(
-        padded[:, :members],
-        padded[:, members],
-        padded[:, members + 1],
-        padded[:, members + 2],
-        offsets,
-        center,
-    )
+    parts = [unpacked(m, members) for m in from_neighbours(packed(*to_next), packed(*to_previous))]
+    gram_sum, innov_sum = (sum(terms) for terms in zip(here, *parts))
     weights = transform_weights(gram_sum, innov_sum, members)
     block = jnp.moveaxis(gathered, 0, 1).reshape(slabs, members, levels, -1)
     analysed = analyse(block, weights)

time: 130 us -> 130 us (level)
  matrix products: 6.26 us -> 10.5 us
  local copies, waits for them, and re-layouts: 7.43 us -> 3.35 us
    dot_general x1 -> x3, matrix products: 0.72 us -> 3.82 us  [local_terms(): jnp.einsum('skn,sjn->skj', scaled, deviations, preferred_element_type=jnp...]
    dot_general x1 -> x3, matrix products: 0.52 us -> 2.82 us  [local_terms(): jnp.einsum('skn,sn->sk', scaled, innovation, preferred_element_type=jnp.f...]
    broadcast_in_dim x4 -> x0, local copies, waits for them, and re-layouts: 2.22 us -> none  [the longest x1 0.77 us: on_device(): obs_innov[:, None, :]]
    dot_general x5 -> x3, matrix products: 3.35 us -> 2.09 us  [matmul(): jnp.einsum('sij,sjk->sik', left, right, precision=lax.Precision.HIGHEST)]
where the time goes in v2:
time: 130 us; the launch traced here: 129 us
  blocking collectives  43.8 us (34%)
  waiting for transfers between devices  36.9 us (28%)
  starting transfers between devices  32.9 us (25%)
  matrix products  10.5 us (8%)
  local copies, waits for them, and re-layouts  3.35 us (3%)
  other arithmetic  1.8 us (1%)
    all_to_all x1, blocking collectives, on_device(): lax.all_to_all(analysed, MEM, split_axis=1, concat_axis=3, tiled=True)  43.8 us
    all_to_all x1, waiting for transfers between devices, on_device(): gathered = lax.all_to_all(pieces, MEM, 0, 0, tiled=True)  36.9 us
    ppermute x1, starting transfers between devices, from_neighbours(): high = lax.ppermute(to_previous, 'patch', backward)  14 us
    all_to_all x1, starting transfers between devices, on_device(): gathered = lax.all_to_all(pieces, MEM, 0, 0, tiled=True)  13.9 us
    ppermute x1, starting transfers between devices, from_neighbours(): low = lax.ppermute(to_next, 'patch', forward)  4.91 us
    dot_general x3, matrix products, local_terms(): jnp.einsum('skn,sjn->skj', scaled, deviations, preferred_element_type=jnp...  3.82 us
    dot_general x3, matrix products, local_terms(): jnp.einsum('skn,sn->sk', scaled, innovation, preferred_element_type=jnp.f...  2.82 us
  transfers between devices with their start and end apart: 3, of which 1 were waited for; matrix products, arithmetic and copies ran while one was open for 7% of the time, Pallas kernels for 0%

profile of v2, /device:TPU:19, one launch (start us, length us, event | category | flops | bytes accessed | tf_op | source)
XLA Modules:
  0.0 129.4 jit_solution(968505096688718331)
XLA Ops:
  0.0 0.0 copy-start
  0.0 0.0 copy-start.1
  0.0 0.0 copy-start.2
  0.0 0.8 convert_multiply_fusion.4
  0.9 1.7 %convolution_convert_fusion.1 = bf16[2,256,256]{2,1,0:T(8,128)(2,1)S(1)} fusion(bf16[2,256,512]{2,1,0:T(8,128)(2,1)} %param.6, f32[2,512]{1,0:T(2,128)S(1)} %get-tuple-element.5), kind=kOutput, calls=%fused_computation.11 | convolution fusion | flops 135135232 | bytes 790528 | tf_op jit(solution)/shard_map/skn,sjn->skj/dot_general | solution.py:31
  2.5 1.3 fusion.10
  3.9 4.9 %collective-permute-start = (bf16[2,264,256]{2,1,0:T(8,128)(2,1)S(1)}, bf16[2,264,256]{2,1,0:T(8,128)(2,1)S(1)}, u32[]{:S(2)}, u32[]{:S(2)}) collective-permute-start(bf16[2,264,256]{2,1,0:T(8,128)(2,1)S(1)} %pad_maximum_fusion), channel_id=1, source_target_pairs={{0,1},{1,2},{2,3},{3,4},{4,5},{5,6},{6,7},{7,8},{8,9},{9,10},{10,1... | collective-permute-start | bytes 811016 | tf_op jit(solution)/shard_map/ppermute | solution.py:17
  8.8 0.0 copy-done.1
  8.8 0.0 copy-done.2
  8.8 0.2 fusion.7
  9.1 0.3 convolution_convert_fusion
  9.5 14.0 %collective-permute-start.1 = (bf16[2,264,256]{2,1,0:T(8,128)(2,1)S(1)}, bf16[2,264,256]{2,1,0:T(8,128)(2,1)S(1)}, u32[]{:S(2)}, u32[]{:S(2)}) collective-permute-start(bf16[2,264,256]{2,1,0:T(8,128)(2,1)S(1)} %pad_maximum_fusion.1), channel_id=1, source_target_pairs={{1,0},{2,1},{3,2},{4,3},{5,4},{6,5},{7,6},{8,7},{9,8},{10,9},{11,1... | collective-permute-start | bytes 811016 | tf_op jit(solution)/shard_map/ppermute | solution.py:18
  23.5 0.0 copy-done
  23.6 1.3 bitcast_bitcast_fusion
  24.8 13.9 %all-to-all-start = ((bf16[64,2,4,8,128]{4,3,2,1,0:T(8,128)(2,1)}), bf16[64,2,4,8,128]{4,3,2,1,0:T(8,128)(2,1)S(1)}, u32[]{:S(2)}, u32[]{:S(2)}) async-start(bf16[64,2,4,8,128]{4,3,2,1,0:T(8,128)(2,1)} %bitcast_bitcast_fusion), calls=%async_computation | async-start | bytes 2097152 | tf_op jit(solution)/shard_map/all_to_all | solution.py:80
  38.8 1.3 fusion.13
  40.1 0.0 collective-permute-done
  40.1 0.0 collective-permute-done.1
  40.1 1.8 %multiply_reduce_fusion = (f32[2]{0:T(128)S(1)}, f32[2,256,256]{2,1,0:T(8,128)S(1)}) fusion(bf16[2,264,256]{2,1,0:T(8,128)(2,1)S(1)} %collective-permute-done.1, bf16[2,264,256]{2,1,0:T(8,128)(2,1)S(1)} %collective-permute-done, f32[256,256]{1,0:T(8,128)S(1)} %fusion.35, bf16[2,256,512]{2,1,0:T(8,128)(2,1)} %param.6, f32[2,512]{1,0:T(2,128)S(1)} %get-tuple-element.7), kind=kOutput, calls=%fused_computation.26 | convolution fusion | flops 135921664 | bytes 2363400 | tf_op jit(solution)/shard_map/skn,sjn->skj/dot_general | solution.py:31
  42.0 0.1 broadcast_divide_fusion
  42.1 0.7 fusion.18
  42.8 0.7 fusion.1
  43.6 0.7 fusion.17
  44.3 0.5 fusion.66
  44.8 0.6 fusion.64
  45.4 0.1 bitcast_divide_fusion
  45.4 36.9 %all-to-all-done = bf16[64,2,4,8,128]{4,3,2,1,0:T(8,128)(2,1)S(1)} async-done(((bf16[64,2,4,8,128]{4,3,2,1,0:T(8,128)(2,1)}), bf16[64,2,4,8,128]{4,3,2,1,0:T(8,128)(2,1)S(1)}, u32[]{:S(2)}, u32[]{:S(2)}) %all-to-all-start) | async-done | bytes 1048608 | tf_op jit(solution)/shard_map/all_to_all | solution.py:80
  82.4 0.3 convert_reduce_fusion
  82.7 0.3 convert_bitcast_fusion
  82.9 0.2 copy.31
  83.2 0.6 add_convert_fusion
  83.8 0.7 copy.34
  84.5 43.8 %all_to_all.23 = bf16[2,256,8,128]{3,2,0,1:T(8,128)(2,1)S(1)} all-to-all(bf16[2,256,8,128]{3,2,0,1:T(8,128)(2,1)S(1)} %copy.34), channel_id=1, replica_groups=mesh['mem'=64,'patch'=16] {'mem'}, dimensions={1} | all-to-all | bytes 2097152 | tf_op jit(solution)/shard_map/all_to_all | solution.py:91
  128.3 1.2 copy.79
  (18 shorter events, 0.2 us)
Async XLA Ops:
  0.0 23.5 %copy-start = (bf16[2,4,8,8192]{3,2,1,0:T(8,128)(2,1)S(1)}, bf16[2,4,8,8192]{3,2,1,0:T(8,128)(2,1)}, u32[]{:S(2)}) copy-start(bf16[2,4,8,8192]{3,2,1,0:T(8,128)(2,1)} %param.5) | copy-start | bytes 3145732
  0.0 8.8 %copy-start.1 = (bf16[2,256,512]{2,1,0:T(8,128)(2,1)S(1)}, bf16[2,256,512]{2,1,0:T(8,128)(2,1)}, u32[]{:S(2)}) copy-start(bf16[2,256,512]{2,1,0:T(8,128)(2,1)} %param.6) | copy-start | bytes 1572868
  0.0 8.8 %copy-start.2 = (bf16[2,512]{1,0:T(2,128)(2,1)S(1)}, bf16[2,512]{1,0:T(2,128)(2,1)}, u32[]{:S(2)}) copy-start(bf16[2,512]{1,0:T(2,128)(2,1)} %param.7) | copy-start | bytes 6148
  3.9 36.2 %collective-permute-start = (bf16[2,264,256]{2,1,0:T(8,128)(2,1)S(1)}, bf16[2,264,256]{2,1,0:T(8,128)(2,1)S(1)}, u32[]{:S(2)}, u32[]{:S(2)}) collective-permute-start(bf16[2,264,256]{2,1,0:T(8,128)(2,1)S(1)} %pad_maximum_fusion), channel_id=1, source_target_pairs={{0,1},{1,2},{2,3},{3,4},{4,5},{5,6},{6,7},{7,8},{8,9},{9,10},{10,1... | collective-permute-start | bytes 811016 | tf_op jit(solution)/shard_map/ppermute | solution.py:17
  9.5 30.6 %collective-permute-start.1 = (bf16[2,264,256]{2,1,0:T(8,128)(2,1)S(1)}, bf16[2,264,256]{2,1,0:T(8,128)(2,1)S(1)}, u32[]{:S(2)}, u32[]{:S(2)}) collective-permute-start(bf16[2,264,256]{2,1,0:T(8,128)(2,1)S(1)} %pad_maximum_fusion.1), channel_id=1, source_target_pairs={{1,0},{2,1},{3,2},{4,3},{5,4},{6,5},{7,6},{8,7},{9,8},{10,9},{11,1... | collective-permute-start | bytes 811016 | tf_op jit(solution)/shard_map/ppermute | solution.py:18
  24.8 57.5 %all-to-all-start = ((bf16[64,2,4,8,128]{4,3,2,1,0:T(8,128)(2,1)}), bf16[64,2,4,8,128]{4,3,2,1,0:T(8,128)(2,1)S(1)}, u32[]{:S(2)}, u32[]{:S(2)}) async-start(bf16[64,2,4,8,128]{4,3,2,1,0:T(8,128)(2,1)} %bitcast_bitcast_fusion), calls=%async_computation | async-start | bytes 2097152 | tf_op jit(solution)/shard_map/all_to_all | solution.py:80

commit v3 on v2

--- a/solution.py
+++ b/solution.py
@@ -8,14 +8,15 @@
 NS_ITERS = 2
 MEM = "mem"
 LOC_SCALE = 0.5
+RUN = 8
+EARLY_ROWS = (0,)
 
 
-def from_neighbours(to_next, to_previous):
+def sent(to_next, to_previous, chosen):
     count = lax.axis_size("patch")
-    forward = [(i, (i + 1) % count) for i in range(count)]
-    backward = [(target, source) for source, target in forward]
-    low = lax.ppermute(to_next, "patch", forward)
-    high = lax.ppermute(to_previous, "patch", backward)
+    sources = [i for i in range(count) if (i % RUN in EARLY_ROWS) == chosen]
+    low = lax.ppermute(to_next, "patch", [(i, (i + 1) % count) for i in sources])
+    high = lax.ppermute(to_previous, "patch", [(i, (i - 1) % count) for i in sources])
     return low, high
 
 
@@ -75,15 +76,18 @@
     slabs, own, levels, _ = ens.shape
     members = obs_pert.shape[1]
     ranks = lax.axis_size(MEM)
-    pieces = jnp.moveaxis(ens.reshape(slabs, own, levels, ranks, -1), 3, 0)
-    pieces = with_layout_constraint(pieces, Layout((0, 1, 2, 3, 4)))
-    gathered = lax.all_to_all(pieces, MEM, 0, 0, tiled=True)
     center = (lax.axis_index(MEM).astype(jnp.float32) + 0.5) / ranks
     here, to_next, to_previous = (
         local_terms(obs_pert, obs_innov, obs_pos, obs_prec, offset, center)
         for offset in (0.0, -1.0, 1.0)
     )
-    parts = [unpacked(m, members) for m in from_neighbours(packed(*to_next), packed(*to_previous))]
+    messages = packed(*to_next), packed(*to_previous)
+    received = sent(*messages, False)
+    pieces = jnp.moveaxis(ens.reshape(slabs, own, levels, ranks, -1), 3, 0)
+    pieces = with_layout_constraint(pieces, Layout((0, 1, 2, 3, 4)))
+    gathered = lax.all_to_all(pieces, MEM, 0, 0, tiled=True)
+    received += sent(*messages, True)
+    parts = [unpacked(message, members) for message in received]
     gram_sum, innov_sum = (sum(terms) for terms in zip(here, *parts))
     weights = transform_weights(gram_sum, innov_sum, members)
     block = jnp.moveaxis(gathered, 0, 1).reshape(slabs, members, levels, -1)

time: 130 us -> 132 us (1.015)
  starting transfers between devices: 32.9 us -> 34.8 us
    ppermute x2 -> x4, starting transfers between devices: 18.9 us -> 20.9 us  [the longest x2 14.7 us: sent(): lax.ppermute(to_previous, 'patch', [(i, (i - 1) % count) for i in sources])]
  transfers between devices with their start and end apart: 3 -> 5, of which waited for: 1 -> 1; matrix products, arithmetic and copies ran while one was open for 7% -> 7% of each run, Pallas kernels for 0% -> 0%
where the time goes in v3:
time: 132 us; the launch traced here: 131 us
  blocking collectives  43.8 us (33%)
  waiting for transfers between devices  36 us (27%)
  starting transfers between devices  34.8 us (26%)
  matrix products  10.8 us (8%)
  local copies, waits for them, and re-layouts  3.35 us (3%)
  other arithmetic  2.39 us (2%)
    all_to_all x1, blocking collectives, on_device(): lax.all_to_all(analysed, MEM, split_axis=1, concat_axis=3, tiled=True)  43.8 us
    all_to_all x1, waiting for transfers between devices, on_device(): gathered = lax.all_to_all(pieces, MEM, 0, 0, tiled=True)  36 us
    ppermute x2, starting transfers between devices, sent(): lax.ppermute(to_previous, 'patch', [(i, (i - 1) % count) for i in sources])  14.7 us
    all_to_all x1, starting transfers between devices, on_device(): gathered = lax.all_to_all(pieces, MEM, 0, 0, tiled=True)  13.9 us
    ppermute x2, starting transfers between devices, sent(): lax.ppermute(to_next, 'patch', [(i, (i + 1) % count) for i in sources])  6.21 us
    dot_general x3, matrix products, local_terms(): jnp.einsum('skn,sjn->skj', scaled, deviations, preferred_element_type=jnp...  3.95 us
    dot_general x3, matrix products, local_terms(): jnp.einsum('skn,sn->sk', scaled, innovation, preferred_element_type=jnp.f...  2.82 us
  transfers between devices with their start and end apart: 5, of which 1 were waited for; matrix products, arithmetic and copies ran while one was open for 7% of the time, Pallas kernels for 0%

profile of v3, /device:TPU:19, one launch (start us, length us, event | category | flops | bytes accessed | tf_op | source)
XLA Modules:
  0.0 131.4 jit_solution(11330690300551508353)
XLA Ops:
  0.0 0.0 copy-start
  0.0 0.0 copy-start.1
  0.0 0.0 copy-start.2
  0.0 0.8 convert_multiply_fusion.5
  0.9 1.7 %convolution_convert_fusion.1 = bf16[2,256,256]{2,1,0:T(8,128)(2,1)S(1)} fusion(bf16[2,256,512]{2,1,0:T(8,128)(2,1)} %param.6, f32[2,512]{1,0:T(2,128)S(1)} %get-tuple-element.8), kind=kOutput, calls=%fused_computation.11 | convolution fusion | flops 135135232 | bytes 790528 | tf_op jit(solution)/shard_map/skn,sjn->skj/dot_general | solution.py:32
  2.5 1.3 fusion.10
  3.9 4.9 %collective-permute-start.2 = (bf16[2,264,256]{2,1,0:T(8,128)(2,1)S(1)}, bf16[2,264,256]{2,1,0:T(8,128)(2,1)S(1)}, u32[]{:S(2)}, u32[]{:S(2)}) collective-permute-start(bf16[2,264,256]{2,1,0:T(8,128)(2,1)S(1)} %pad_maximum_fusion), channel_id=1, source_target_pairs={{0,1},{8,9},{16,17},{24,25},{32,33},{40,41},{48,49},{56,57},{64,65... | collective-permute-start | bytes 811016 | tf_op jit(solution)/shard_map/ppermute | solution.py:18
  8.8 1.3 collective-permute-start
  10.1 0.0 copy-done.1
  10.1 0.0 copy-done.2
  10.1 0.2 fusion.7
  10.4 0.3 convolution_convert_fusion
  10.8 13.4 %collective-permute-start.3 = (bf16[2,264,256]{2,1,0:T(8,128)(2,1)S(1)}, bf16[2,264,256]{2,1,0:T(8,128)(2,1)S(1)}, u32[]{:S(2)}, u32[]{:S(2)}) collective-permute-start(bf16[2,264,256]{2,1,0:T(8,128)(2,1)S(1)} %pad_maximum_fusion.1), channel_id=1, source_target_pairs={{0,15},{8,7},{16,31},{24,23},{32,47},{40,39},{48,63},{56,55},{64,7... | collective-permute-start | bytes 811016 | tf_op jit(solution)/shard_map/ppermute | solution.py:19
  24.2 1.3 collective-permute-start.1
  25.5 0.0 copy-done
  25.6 1.3 bitcast_bitcast_fusion
  26.8 13.9 %all-to-all-start = ((bf16[64,2,4,8,128]{4,3,2,1,0:T(8,128)(2,1)}), bf16[64,2,4,8,128]{4,3,2,1,0:T(8,128)(2,1)S(1)}, u32[]{:S(2)}, u32[]{:S(2)}) async-start(bf16[64,2,4,8,128]{4,3,2,1,0:T(8,128)(2,1)} %bitcast_bitcast_fusion), calls=%async_computation | async-start | bytes 2097152 | tf_op jit(solution)/shard_map/all_to_all | solution.py:88
  40.8 1.3 fusion.13
  42.1 0.0 collective-permute-done.2
  42.1 0.0 collective-permute-done
  42.2 0.0 collective-permute-done.3
  42.2 0.0 collective-permute-done.1
  42.2 1.9 %multiply_reduce_fusion = (f32[2]{0:T(128)S(1)}, f32[2,256,256]{2,1,0:T(8,128)S(1)}) fusion(bf16[2,264,256]{2,1,0:T(8,128)(2,1)S(1)} %collective-permute-done.3, bf16[2,264,256]{2,1,0:T(8,128)(2,1)S(1)} %collective-permute-done.2, bf16[2,264,256]{2,1,0:T(8,128)(2,1)} %collective-permute-done.1, bf16[2,264,256]{2,1,0:T(8,128)(2,1)S(1)} %collective-permute-done, ...), kind=kOutput, calls=%fused_computation.26 | convolution fusion | flops 136445952 | bytes 2887688 | tf_op jit(solution)/shard_map/skn,sjn->skj/dot_general | solution.py:32
  44.2 0.7 convert_reduce_fusion.3
  44.9 0.8 fusion.18
  45.7 0.7 fusion.1
  46.4 0.8 fusion.17
  47.2 0.5 fusion.68
  47.8 0.6 fusion.66
  48.3 0.1 bitcast_divide_fusion
  48.4 36.0 %all-to-all-done = bf16[64,2,4,8,128]{4,3,2,1,0:T(8,128)(2,1)S(1)} async-done(((bf16[64,2,4,8,128]{4,3,2,1,0:T(8,128)(2,1)}), bf16[64,2,4,8,128]{4,3,2,1,0:T(8,128)(2,1)S(1)}, u32[]{:S(2)}, u32[]{:S(2)}) %all-to-all-start) | async-done | bytes 1048608 | tf_op jit(solution)/shard_map/all_to_all | solution.py:88
  84.4 0.3 convert_reduce_fusion
  84.6 0.3 convert_bitcast_fusion
  84.9 0.2 copy.31
  85.2 0.6 add_convert_fusion
  85.8 0.7 copy.34
  86.5 43.8 %all_to_all.23 = bf16[2,256,8,128]{3,2,0,1:T(8,128)(2,1)S(1)} all-to-all(bf16[2,256,8,128]{3,2,0,1:T(8,128)(2,1)S(1)} %copy.34), channel_id=1, replica_groups=mesh['mem'=64,'patch'=16] {'mem'}, dimensions={1} | all-to-all | bytes 2097152 | tf_op jit(solution)/shard_map/all_to_all | solution.py:95
  130.2 1.2 copy.79
  (19 shorter events, 0.2 us)
Async XLA Ops:
  0.0 25.5 %copy-start = (bf16[2,4,8,8192]{3,2,1,0:T(8,128)(2,1)S(1)}, bf16[2,4,8,8192]{3,2,1,0:T(8,128)(2,1)}, u32[]{:S(2)}) copy-start(bf16[2,4,8,8192]{3,2,1,0:T(8,128)(2,1)} %param.5) | copy-start | bytes 3145732
  0.0 10.1 %copy-start.1 = (bf16[2,256,512]{2,1,0:T(8,128)(2,1)S(1)}, bf16[2,256,512]{2,1,0:T(8,128)(2,1)}, u32[]{:S(2)}) copy-start(bf16[2,256,512]{2,1,0:T(8,128)(2,1)} %param.6) | copy-start | bytes 1572868
  0.0 10.1 %copy-start.2 = (bf16[2,512]{1,0:T(2,128)(2,1)S(1)}, bf16[2,512]{1,0:T(2,128)(2,1)}, u32[]{:S(2)}) copy-start(bf16[2,512]{1,0:T(2,128)(2,1)} %param.7) | copy-start | bytes 6148
  3.9 38.2 %collective-permute-start.2 = (bf16[2,264,256]{2,1,0:T(8,128)(2,1)S(1)}, bf16[2,264,256]{2,1,0:T(8,128)(2,1)S(1)}, u32[]{:S(2)}, u32[]{:S(2)}) collective-permute-start(bf16[2,264,256]{2,1,0:T(8,128)(2,1)S(1)} %pad_maximum_fusion), channel_id=1, source_target_pairs={{0,1},{8,9},{16,17},{24,25},{32,33},{40,41},{48,49},{56,57},{64,65... | collective-permute-start | bytes 811016 | tf_op jit(solution)/shard_map/ppermute | solution.py:18
  8.8 33.3 %collective-permute-start = (bf16[2,264,256]{2,1,0:T(8,128)(2,1)S(1)}, bf16[2,264,256]{2,1,0:T(8,128)(2,1)S(1)}, u32[]{:S(2)}, u32[]{:S(2)}) collective-permute-start(bf16[2,264,256]{2,1,0:T(8,128)(2,1)S(1)} %pad_maximum_fusion), channel_id=1, source_target_pairs={{1,2},{2,3},{3,4},{4,5},{5,6},{6,7},{7,8},{9,10},{10,11},{11,12},{... | collective-permute-start | bytes 811016 | tf_op jit(solution)/shard_map/ppermute | solution.py:18
  10.8 31.3 %collective-permute-start.3 = (bf16[2,264,256]{2,1,0:T(8,128)(2,1)S(1)}, bf16[2,264,256]{2,1,0:T(8,128)(2,1)S(1)}, u32[]{:S(2)}, u32[]{:S(2)}) collective-permute-start(bf16[2,264,256]{2,1,0:T(8,128)(2,1)S(1)} %pad_maximum_fusion.1), channel_id=1, source_target_pairs={{0,15},{8,7},{16,31},{24,23},{32,47},{40,39},{48,63},{56,55},{64,7... | collective-permute-start | bytes 811016 | tf_op jit(solution)/shard_map/ppermute | solution.py:19
  24.2 18.0 %collective-permute-start.1 = (bf16[2,264,256]{2,1,0:T(8,128)(2,1)S(1)}, bf16[2,264,256]{2,1,0:T(8,128)(2,1)}, u32[]{:S(2)}, u32[]{:S(2)}) collective-permute-start(bf16[2,264,256]{2,1,0:T(8,128)(2,1)S(1)} %pad_maximum_fusion.1), channel_id=1, source_target_pairs={{1,0},{2,1},{3,2},{4,3},{5,4},{6,5},{7,6},{9,8},{10,9},{11,10},{12... | collective-permute-start | bytes 811016 | tf_op jit(solution)/shard_map/ppermute | solution.py:19
  26.8 57.5 %all-to-all-start = ((bf16[64,2,4,8,128]{4,3,2,1,0:T(8,128)(2,1)}), bf16[64,2,4,8,128]{4,3,2,1,0:T(8,128)(2,1)S(1)}, u32[]{:S(2)}, u32[]{:S(2)}) async-start(bf16[64,2,4,8,128]{4,3,2,1,0:T(8,128)(2,1)} %bitcast_bitcast_fusion), calls=%async_computation | async-start | bytes 2097152 | tf_op jit(solution)/shard_map/all_to_all | solution.py:88

commit v4 on v3

v4 whole, which is shorter than its diff:
```python
import functools

import jax
import jax.numpy as jnp
from jax import lax
from jax.experimental import pallas as pl
from jax.experimental.pallas import tpu as pltpu
from jax.experimental.layout import Layout, with_layout_constraint
from jax.sharding import PartitionSpec as P


NS_ITERS = 2
MEM = "mem"
LOC_SCALE = 0.5
RUN = 8
EARLY_ROWS = (0,)


def sent(to_next, to_previous, chosen):
    count = lax.axis_size("patch")
    sources = [i for i in range(count) if (i % RUN in EARLY_ROWS) == chosen]
    low = lax.ppermute(to_next, "patch", [(i, (i + 1) % count) for i in sources])
    high = lax.ppermute(to_previous, "patch", [(i, (i - 1) % count) for i in sources])
    return low, high


def region_sums(extended, deviations, position, precision, offset, center, dtype):
    distance = position.astype(jnp.float32) + offset - center
    taper = jnp.exp(-0.5 * (distance / LOC_SCALE) ** 2)
    obs_weight = taper * precision.astype(jnp.float32)
    scaled = (deviations.astype(jnp.float32) * obs_weight[:, None, :]).astype(jnp.bfloat16)
    sums = jnp.einsum("sjn,skn->sjk", extended, scaled, preferred_element_type=jnp.float32)
    return sums.astype(dtype)


def matmul(left, right):
    return jnp.dot(left, right, precision=lax.Precision.HIGHEST, preferred_element_type=jnp.float32)


def matmul_t(left, right):
    return lax.dot_general(
        left,
        right,
        (((1,), (1,)), ((), ())),
        precision=lax.Precision.HIGHEST,
        preferred_element_type=jnp.float32,
    )


def slab_weights(sums, members):
    rows = lax.broadcasted_iota(jnp.int32, (members, members), 0)
    columns = lax.broadcasted_iota(jnp.int32, (members, members), 1)
    identity = jnp.where(rows == columns, 1.0, 0.0).astype(jnp.float32)
    system = (members - 1.0) * identity + sums[:members]
    frobenius = jnp.sqrt(jnp.sum(jnp.sum(system * system, axis=1, keepdims=True), axis=0, keepdims=True))
    current = system / frobenius
    inverse = 1.5 * identity - 0.5 * current
    factor = inverse
    for _ in range(1, NS_ITERS):
        current = matmul(current, factor)
        factor = 1.5 * identity - 0.5 * matmul(inverse, current)
        inverse = matmul(factor, inverse)
    inner = matmul_t(sums[members:], inverse)
    mean_weight = matmul_t(inverse, inner)[:, :1] / frobenius
    return (inverse * jnp.sqrt((members - 1.0) / frobenius) + mean_weight).astype(jnp.bfloat16)


def transform_weights(own, messages, earlier, late_rows):
    slabs, _, members = own.shape

    def kernel(*refs):
        own_ref, message_refs, out_ref = refs[0], refs[1 : 1 + len(messages)], refs[-1]

        def compute():
            for s in range(slabs):
                sums = own_ref[s]
                for ref in message_refs:
                    sums = sums + ref[s].astype(jnp.float32)
                out_ref[s] = slab_weights(sums, members)

        if earlier is None:
            compute()
        else:
            late = lax.axis_index("patch") % RUN
            arrives = functools.reduce(lambda a, b: a & b, [late != row for row in late_rows])
            pl.when(arrives)(compute)

            @pl.when(jnp.logical_not(arrives))
            def _():
                out_ref[...] = refs[-2][...]

    operands = (own, *messages) + (() if earlier is None else (earlier,))
    return pl.pallas_call(
        kernel,
        out_shape=jax.ShapeDtypeStruct((slabs, members, members), jnp.bfloat16),
        compiler_params=pltpu.CompilerParams(vmem_limit_bytes=16 * 2**20),
        name="weights" if earlier is None else "weights_again",
    )(*operands)


def analyse(block, weights):
    average = jnp.mean(block.astype(jnp.float32), axis=1, keepdims=True)
    anomaly = (block.astype(jnp.float32) - average).astype(jnp.bfloat16)
    mixed = jnp.einsum("sjlg,sjk->sklg", anomaly, weights, preferred_element_type=jnp.float32)
    return (average + mixed).astype(jnp.bfloat16)


def on_device(ens, obs_pert, obs_innov, obs_pos, obs_prec):
    slabs, own, levels, _ = ens.shape
    members = obs_pert.shape[1]
    ranks = lax.axis_size(MEM)
    center = (lax.axis_index(MEM).astype(jnp.float32) + 0.5) / ranks
    rows = jnp.pad(obs_innov[:, None, :], ((0, 0), (0, 7), (0, 0)))
    extended = jnp.concatenate([obs_pert, rows], axis=1)

    def sums(offset, dtype):
        return region_sums(extended, obs_pert, obs_pos, obs_prec, offset, center, dtype)

    messages = sums(-1.0, jnp.bfloat16), sums(1.0, jnp.bfloat16)
    received = sent(*messages, False)
    pieces = jnp.moveaxis(ens.reshape(slabs, own, levels, ranks, -1), 3, 0)
    pieces = with_layout_constraint(pieces, Layout((0, 1, 2, 3, 4)))
    gathered = lax.all_to_all(pieces, MEM, 0, 0, tiled=True)
    late = sent(*messages, True)
    own_sums = sums(0.0, jnp.float32)
    weights = transform_weights(own_sums, received, None, EARLY_ROWS)
    weights = transform_weights(own_sums, received + late, weights, EARLY_ROWS)
    block = jnp.moveaxis(gathered, 0, 1).reshape(slabs, members, levels, -1)
    analysed = analyse(block, weights)
    return lax.all_to_all(analysed, MEM, split_axis=1, concat_axis=3, tiled=True)


def solution(mesh):
    return jax.shard_map(
        on_device,
        mesh=mesh,
        in_specs=(
            P(None, MEM, None, "patch"),
            P(None, None, "patch"),
            P(None, "patch"),
            P(None, "patch"),
            P(None, "patch"),
        ),
        out_specs=P(None, MEM, None, "patch"),
        check_vma=False,
    )
```

time: 132 us -> 115 us (0.87)
  the two profiles are of different devices: /device:TPU:19 before, /device:TPU:1 now
where the time goes in v4:
time: 115 us
  blocking collectives  43.9 us (38%)
  starting transfers between devices  37.7 us (33%)
  waiting for transfers between devices  21.2 us (18%)
  Pallas kernels  4.73 us (4%)
  local copies, waits for them, and re-layouts  4.56 us (4%)
  matrix products  1.62 us (1%)
    all_to_all x1, blocking collectives, on_device(): lax.all_to_all(analysed, MEM, split_axis=1, concat_axis=3, tiled=True)  43.9 us
    ppermute x2, waiting for transfers between devices, sent(): lax.ppermute(to_next, 'patch', [(i, (i + 1) % count) for i in sources])  21.2 us
    all_to_all x1, starting transfers between devices, on_device(): gathered = lax.all_to_all(pieces, MEM, 0, 0, tiled=True)  18.3 us
    ppermute x2, starting transfers between devices, sent(): lax.ppermute(to_previous, 'patch', [(i, (i - 1) % count) for i in sources])  12.6 us
    ppermute x2, starting transfers between devices, sent(): lax.ppermute(to_next, 'patch', [(i, (i + 1) % count) for i in sources])  6.79 us
    pallas_call x2, Pallas kernels, transform_weights(): pl.pallas_call(kernel, out_shape=jax.ShapeDtypeStruct((slabs, members, me...  4.73 us
  transfers between devices with their start and end apart: 5, of which 1 were waited for; matrix products, arithmetic and copies ran while one was open for 1% of the time, Pallas kernels for 4%

profile of v4, /device:TPU:1, one launch (start us, length us, event | category | flops | bytes accessed | tf_op | source)
XLA Modules:
  0.0 114.5 jit_solution(15034300384862734142)
XLA Ops:
  0.0 0.0 copy-start
  0.0 1.2 %copy-done = bf16[2,4,8,8192]{3,2,1,0:T(8,128)(2,1)S(1)} copy-done((bf16[2,4,8,8192]{3,2,1,0:T(8,128)(2,1)S(1)}, bf16[2,4,8,8192]{3,2,1,0:T(8,128)(2,1)}, u32[]{:S(2)}) %copy-start) | copy-done | bytes 1048600
  1.2 1.3 %bitcast_bitcast_fusion = bf16[64,2,4,8,128]{4,3,2,1,0:T(8,128)(2,1)} fusion(bf16[2,4,8,8192]{3,2,1,0:T(8,128)(2,1)S(1)} %copy-done), kind=kLoop, calls=%fused_computation.15 | loop fusion | bytes 2097152 | tf_op jit(solution)/shard_map/transpose | solution.py:121
  2.5 0.0 copy-start.1
  2.5 0.0 copy-start.2
  2.5 0.0 copy-start.3
  2.5 0.0 copy-start.4
  2.5 18.3 %all-to-all-start = ((bf16[64,2,4,8,128]{4,3,2,1,0:T(8,128)(2,1)}), bf16[64,2,4,8,128]{4,3,2,1,0:T(8,128)(2,1)S(1)}, u32[]{:S(2)}, u32[]{:S(2)}) async-start(bf16[64,2,4,8,128]{4,3,2,1,0:T(8,128)(2,1)} %bitcast_bitcast_fusion), calls=%async_computation | async-start | bytes 2097152 | tf_op jit(solution)/shard_map/all_to_all | solution.py:123
  20.9 0.0 copy-done.1
  20.9 0.0 copy-done.2
  20.9 0.0 copy-done.3
  20.9 0.0 copy-done.4
  21.0 0.4 convolution_convert_fusion.1
  21.3 1.3 %collective-permute-start = (bf16[2,264,256]{2,1,0:T(8,128)(2,1)S(1)}, bf16[2,264,256]{2,1,0:T(8,128)(2,1)S(1)}, u32[]{:S(2)}, u32[]{:S(2)}) collective-permute-start(bf16[2,264,256]{2,1,0:T(8,128)(2,1)S(1)} %convolution_convert_fusion.1), channel_id=1, source_target_pairs={{1,2},{2,3},{3,4},{4,5},{5,6},{6,7},{7,8},{9,10},{10,11},{11,12},{... | collective-permute-start | bytes 811016 | tf_op jit(solution)/shard_map/ppermute | solution.py:22
  22.6 0.4 convolution_convert_fusion
  23.0 1.3 %collective-permute-start.1 = (bf16[2,264,256]{2,1,0:T(8,128)(2,1)S(1)}, bf16[2,264,256]{2,1,0:T(8,128)(2,1)S(1)}, u32[]{:S(2)}, u32[]{:S(2)}) collective-permute-start(bf16[2,264,256]{2,1,0:T(8,128)(2,1)S(1)} %convolution_convert_fusion), channel_id=1, source_target_pairs={{1,0},{2,1},{3,2},{4,3},{5,4},{6,5},{7,6},{9,8},{10,9},{11,10},{12... | collective-permute-start | bytes 811016 | tf_op jit(solution)/shard_map/ppermute | solution.py:23
  24.3 5.5 %collective-permute-start.2 = (bf16[2,264,256]{2,1,0:T(8,128)(2,1)S(1)}, bf16[2,264,256]{2,1,0:T(8,128)(2,1)S(1)}, u32[]{:S(2)}, u32[]{:S(2)}) collective-permute-start(bf16[2,264,256]{2,1,0:T(8,128)(2,1)S(1)} %convolution_convert_fusion.1), channel_id=1, source_target_pairs={{0,1},{8,9},{16,17},{24,25},{32,33},{40,41},{48,49},{56,57},{64,65... | collective-permute-start | bytes 811016 | tf_op jit(solution)/shard_map/ppermute | solution.py:22
  29.8 11.3 %collective-permute-start.3 = (bf16[2,264,256]{2,1,0:T(8,128)(2,1)S(1)}, bf16[2,264,256]{2,1,0:T(8,128)(2,1)S(1)}, u32[]{:S(2)}, u32[]{:S(2)}) collective-permute-start(bf16[2,264,256]{2,1,0:T(8,128)(2,1)S(1)} %convolution_convert_fusion), channel_id=1, source_target_pairs={{0,15},{8,7},{16,31},{24,23},{32,47},{40,39},{48,63},{56,55},{64,7... | collective-permute-start | bytes 811016 | tf_op jit(solution)/shard_map/ppermute | solution.py:23
  41.1 0.3 fusion.10.refs_0_
  41.4 21.2 %collective-permute-done.refs_1_ = bf16[2,264,256]{2,1,0:T(8,128)(2,1)S(1)} collective-permute-done((bf16[2,264,256]{2,1,0:T(8,128)(2,1)S(1)}, bf16[2,264,256]{2,1,0:T(8,128)(2,1)S(1)}, u32[]{:S(2)}, u32[]{:S(2)}) %collective-permute-start) | collective-permute-done | bytes 270368 | tf_op jit(solution)/shard_map/ppermute | solution.py:22
  62.6 0.0 collective-permute-done.1.refs_2_
  62.6 4.7 %weights.1.refs_5_ = bf16[2,256,256]{2,1,0:T(8,128)(2,1)S(1)} custom-call(f32[2,264,256]{2,1,0:T(8,128)S(1)} %fusion.10.refs_0_, bf16[2,264,256]{2,1,0:T(8,128)(2,1)S(1)} %collective-permute-done.refs_1_, bf16[2,264,256]{2,1,0:T(8,128)(2,1)S(1)} %collective-permute-done.1.refs_2_), custom_call_target="tpu_custom_call" | custom-call | tf_op jit(solution)/shard_map/weights/pallas_call | solution.py:93
  67.3 0.0 collective-permute-done.2.refs_3_
  67.3 0.0 collective-permute-done.3.refs_4_
  67.4 0.0 all-to-all-done
  67.4 0.3 convert_reduce_fusion
  67.7 0.3 convert_bitcast_fusion
  68.0 0.2 copy.16
  68.2 0.6 add_convert_fusion
  68.8 0.7 copy.19
  69.4 43.9 %all_to_all.23 = bf16[2,256,8,128]{3,2,0,1:T(8,128)(2,1)S(1)} all-to-all(bf16[2,256,8,128]{3,2,0,1:T(8,128)(2,1)S(1)} %copy.19), channel_id=1, replica_groups=mesh['mem'=64,'patch'=16] {'mem'}, dimensions={1} | all-to-all | bytes 2097152 | tf_op jit(solution)/shard_map/all_to_all | solution.py:130
  113.4 1.2 %copy.31 = bf16[2,4,8,64,128]{4,2,3,1,0:T(8,128)(2,1)} copy(bf16[2,4,8,64,128]{4,2,0,1,3:T(8,128)(2,1)S(1)} %bitcast.23) | data formatting | bytes 2097152 | tf_op jit(solution)/shard_map/all_to_all | solution.py:130
  (4 shorter events, 0.1 us)
Async XLA Ops:
  0.0 1.2 %copy-start = (bf16[2,4,8,8192]{3,2,1,0:T(8,128)(2,1)S(1)}, bf16[2,4,8,8192]{3,2,1,0:T(8,128)(2,1)}, u32[]{:S(2)}) copy-start(bf16[2,4,8,8192]{3,2,1,0:T(8,128)(2,1)} %param.5) | copy-start | bytes 3145732
  2.5 18.4 %copy-start.1 = (bf16[2,512]{1,0:T(2,128)(2,1)S(1)}, bf16[2,512]{1,0:T(2,128)(2,1)}, u32[]{:S(2)}) copy-start(bf16[2,512]{1,0:T(2,128)(2,1)} %param.7) | copy-start | bytes 6148
  2.5 18.4 %copy-start.2 = (bf16[2,512]{1,0:T(2,128)(2,1)S(1)}, bf16[2,512]{1,0:T(2,128)(2,1)}, u32[]{:S(2)}) copy-start(bf16[2,512]{1,0:T(2,128)(2,1)} %param.9) | copy-start | bytes 6148
  2.5 18.4 %copy-start.3 = (bf16[2,512]{1,0:T(2,128)(2,1)S(1)}, bf16[2,512]{1,0:T(2,128)(2,1)}, u32[]{:S(2)}) copy-start(bf16[2,512]{1,0:T(2,128)(2,1)} %param.8) | copy-start | bytes 6148
  2.5 18.4 %copy-start.4 = (bf16[2,256,512]{2,1,0:T(8,128)(2,1)S(1)}, bf16[2,256,512]{2,1,0:T(8,128)(2,1)}, u32[]{:S(2)}) copy-start(bf16[2,256,512]{2,1,0:T(8,128)(2,1)} %param.6) | copy-start | bytes 1572868
  2.5 64.9 %all-to-all-start = ((bf16[64,2,4,8,128]{4,3,2,1,0:T(8,128)(2,1)}), bf16[64,2,4,8,128]{4,3,2,1,0:T(8,128)(2,1)S(1)}, u32[]{:S(2)}, u32[]{:S(2)}) async-start(bf16[64,2,4,8,128]{4,3,2,1,0:T(8,128)(2,1)} %bitcast_bitcast_fusion), calls=%async_computation | async-start | bytes 2097152 | tf_op jit(solution)/shard_map/all_to_all | solution.py:123
  21.3 41.3 %collective-permute-start = (bf16[2,264,256]{2,1,0:T(8,128)(2,1)S(1)}, bf16[2,264,256]{2,1,0:T(8,128)(2,1)S(1)}, u32[]{:S(2)}, u32[]{:S(2)}) collective-permute-start(bf16[2,264,256]{2,1,0:T(8,128)(2,1)S(1)} %convolution_convert_fusion.1), channel_id=1, source_target_pairs={{1,2},{2,3},{3,4},{4,5},{5,6},{6,7},{7,8},{9,10},{10,11},{11,12},{... | collective-permute-start | bytes 811016 | tf_op jit(solution)/shard_map/ppermute | solution.py:22
  23.0 39.7 %collective-permute-start.1 = (bf16[2,264,256]{2,1,0:T(8,128)(2,1)S(1)}, bf16[2,264,256]{2,1,0:T(8,128)(2,1)S(1)}, u32[]{:S(2)}, u32[]{:S(2)}) collective-permute-start(bf16[2,264,256]{2,1,0:T(8,128)(2,1)S(1)} %convolution_convert_fusion), channel_id=1, source_target_pairs={{1,0},{2,1},{3,2},{4,3},{5,4},{6,5},{7,6},{9,8},{10,9},{11,10},{12... | collective-permute-start | bytes 811016 | tf_op jit(solution)/shard_map/ppermute | solution.py:23
  24.3 43.1 %collective-permute-start.2 = (bf16[2,264,256]{2,1,0:T(8,128)(2,1)S(1)}, bf16[2,264,256]{2,1,0:T(8,128)(2,1)S(1)}, u32[]{:S(2)}, u32[]{:S(2)}) collective-permute-start(bf16[2,264,256]{2,1,0:T(8,128)(2,1)S(1)} %convolution_convert_fusion.1), channel_id=1, source_target_pairs={{0,1},{8,9},{16,17},{24,25},{32,33},{40,41},{48,49},{56,57},{64,65... | collective-permute-start | bytes 811016 | tf_op jit(solution)/shard_map/ppermute | solution.py:22
  29.8 37.6 %collective-permute-start.3 = (bf16[2,264,256]{2,1,0:T(8,128)(2,1)S(1)}, bf16[2,264,256]{2,1,0:T(8,128)(2,1)S(1)}, u32[]{:S(2)}, u32[]{:S(2)}) collective-permute-start(bf16[2,264,256]{2,1,0:T(8,128)(2,1)S(1)} %convolution_convert_fusion), channel_id=1, source_target_pairs={{0,15},{8,7},{16,31},{24,23},{32,47},{40,39},{48,63},{56,55},{64,7... | collective-permute-start | bytes 811016 | tf_op jit(solution)/shard_map/ppermute | solution.py:23

commit v5 on v4

--- a/solution.py
+++ b/solution.py
@@ -16,12 +16,10 @@
 EARLY_ROWS = (0,)
 
 
-def sent(to_next, to_previous, chosen):
+def sent(message, step, late):
     count = lax.axis_size("patch")
-    sources = [i for i in range(count) if (i % RUN in EARLY_ROWS) == chosen]
-    low = lax.ppermute(to_next, "patch", [(i, (i + 1) % count) for i in sources])
-    high = lax.ppermute(to_previous, "patch", [(i, (i - 1) % count) for i in sources])
-    return low, high
+    sources = [i for i in range(count) if (i % RUN in EARLY_ROWS) == late]
+    return lax.ppermute(message, "patch", [(i, (i + step) % count) for i in sources])
 
 
 def region_sums(extended, deviations, position, precision, offset, center, dtype):
@@ -110,21 +108,26 @@
     members = obs_pert.shape[1]
     ranks = lax.axis_size(MEM)
     center = (lax.axis_index(MEM).astype(jnp.float32) + 0.5) / ranks
-    rows = jnp.pad(obs_innov[:, None, :], ((0, 0), (0, 7), (0, 0)))
+    rows = jnp.broadcast_to(obs_innov[:, None, :], (slabs, 8, obs_innov.shape[1]))
     extended = jnp.concatenate([obs_pert, rows], axis=1)
 
     def sums(offset, dtype):
         return region_sums(extended, obs_pert, obs_pos, obs_prec, offset, center, dtype)
 
-    messages = sums(-1.0, jnp.bfloat16), sums(1.0, jnp.bfloat16)
-    received = sent(*messages, False)
+    to_next = sums(-1.0, jnp.bfloat16)
+    low_first = sent(to_next, 1, False)
     pieces = jnp.moveaxis(ens.reshape(slabs, own, levels, ranks, -1), 3, 0)
     pieces = with_layout_constraint(pieces, Layout((0, 1, 2, 3, 4)))
     gathered = lax.all_to_all(pieces, MEM, 0, 0, tiled=True)
-    late = sent(*messages, True)
+    to_previous = sums(1.0, jnp.bfloat16)
+    high_first = sent(to_previous, -1, False)
+    low_late = sent(to_next, 1, True)
+    high_late = sent(to_previous, -1, True)
     own_sums = sums(0.0, jnp.float32)
+    received = low_first, high_first
     weights = transform_weights(own_sums, received, None, EARLY_ROWS)
-    weights = transform_weights(own_sums, received + late, weights, EARLY_ROWS)
+    received += low_late, high_late
+    weights = transform_weights(own_sums, received, weights, EARLY_ROWS)
     block = jnp.moveaxis(gathered, 0, 1).reshape(slabs, members, levels, -1)
     analysed = analyse(block, weights)
     return lax.all_to_all(analysed, MEM, split_axis=1, concat_axis=3, tiled=True)

time: 115 us -> 115 us (level)
  starting transfers between devices: 37.7 us -> 36.1 us
  waiting for transfers between devices: 21.2 us -> 22.7 us
    ppermute x4, waiting for transfers between devices: 21.2 us -> 22.7 us  [sent(): lax.ppermute(message, 'patch', [(i, (i + step) % count) for i in sources])]
    ppermute x4, starting transfers between devices: 19.4 us -> 17.9 us  [sent(): lax.ppermute(message, 'patch', [(i, (i + step) % count) for i in sources])]
where the time goes in v5:
time: 115 us; the launch traced here: 114 us
  blocking collectives  43.9 us (38%)
  starting transfers between devices  36.1 us (31%)
  waiting for transfers between devices  22.7 us (20%)
  Pallas kernels  4.72 us (4%)
  local copies, waits for them, and re-layouts  4.54 us (4%)
  matrix products  1.6 us (1%)
    all_to_all x1, blocking collectives, on_device(): lax.all_to_all(analysed, MEM, split_axis=1, concat_axis=3, tiled=True)  43.9 us
    ppermute x4, waiting for transfers between devices, sent(): lax.ppermute(message, 'patch', [(i, (i + step) % count) for i in sources])  22.7 us
    all_to_all x1, starting transfers between devices, on_device(): gathered = lax.all_to_all(pieces, MEM, 0, 0, tiled=True)  18.2 us
    ppermute x4, starting transfers between devices, sent(): lax.ppermute(message, 'patch', [(i, (i + step) % count) for i in sources])  17.9 us
    pallas_call x2, Pallas kernels, transform_weights(): pl.pallas_call(kernel, out_shape=jax.ShapeDtypeStruct((slabs, members, me...  4.72 us
  transfers between devices with their start and end apart: 5, of which 1 were waited for; matrix products, arithmetic and copies ran while one was open for 1% of the time, Pallas kernels for 4%

profile of v5, /device:TPU:1, one launch (start us, length us, event | category | flops | bytes accessed | tf_op | source)
XLA Modules:
  0.0 114.4 jit_solution(5718990943337613130)
XLA Ops:
  0.0 0.0 copy-start
  0.0 0.0 copy-start.1
  0.0 0.0 copy-start.2
  0.0 0.0 copy-start.4
  0.0 1.2 %copy-done = bf16[2,4,8,8192]{3,2,1,0:T(8,128)(2,1)S(1)} copy-done((bf16[2,4,8,8192]{3,2,1,0:T(8,128)(2,1)S(1)}, bf16[2,4,8,8192]{3,2,1,0:T(8,128)(2,1)}, u32[]{:S(2)}) %copy-start) | copy-done | bytes 1048600
  1.2 0.0 copy-start.3
  1.2 1.3 %bitcast_bitcast_fusion = bf16[64,2,4,8,128]{4,3,2,1,0:T(8,128)(2,1)} fusion(bf16[2,4,8,8192]{3,2,1,0:T(8,128)(2,1)S(1)} %copy-done), kind=kLoop, calls=%fused_computation.13 | loop fusion | bytes 2097152 | tf_op jit(solution)/shard_map/transpose | solution.py:119
  2.5 18.2 %all-to-all-start = ((bf16[64,2,4,8,128]{4,3,2,1,0:T(8,128)(2,1)}), bf16[64,2,4,8,128]{4,3,2,1,0:T(8,128)(2,1)S(1)}, u32[]{:S(2)}, u32[]{:S(2)}) async-start(bf16[64,2,4,8,128]{4,3,2,1,0:T(8,128)(2,1)} %bitcast_bitcast_fusion), calls=%async_computation | async-start | bytes 2097152 | tf_op jit(solution)/shard_map/all_to_all | solution.py:121
  20.7 0.0 copy-done.1
  20.7 0.0 copy-done.2
  20.8 0.0 copy-done.3
  20.8 0.0 copy-done.4
  20.8 0.3 convolution_convert_fusion
  21.2 1.3 %collective-permute-start.1 = (bf16[2,264,256]{2,1,0:T(8,128)(2,1)S(1)}, bf16[2,264,256]{2,1,0:T(8,128)(2,1)S(1)}, u32[]{:S(2)}, u32[]{:S(2)}) collective-permute-start(bf16[2,264,256]{2,1,0:T(8,128)(2,1)S(1)} %convolution_convert_fusion), channel_id=1, source_target_pairs={{1,0},{2,1},{3,2},{4,3},{5,4},{6,5},{7,6},{9,8},{10,9},{11,10},{12... | collective-permute-start | bytes 811016 | tf_op jit(solution)/shard_map/ppermute | solution.py:22
  22.5 0.3 convolution_convert_fusion.1
  22.8 1.3 %collective-permute-start = (bf16[2,264,256]{2,1,0:T(8,128)(2,1)S(1)}, bf16[2,264,256]{2,1,0:T(8,128)(2,1)S(1)}, u32[]{:S(2)}, u32[]{:S(2)}) collective-permute-start(bf16[2,264,256]{2,1,0:T(8,128)(2,1)S(1)} %convolution_convert_fusion.1), channel_id=1, source_target_pairs={{1,2},{2,3},{3,4},{4,5},{5,6},{6,7},{7,8},{9,10},{10,11},{11,12},{... | collective-permute-start | bytes 811016 | tf_op jit(solution)/shard_map/ppermute | solution.py:22
  24.1 14.0 %collective-permute-start.3 = (bf16[2,264,256]{2,1,0:T(8,128)(2,1)S(1)}, bf16[2,264,256]{2,1,0:T(8,128)(2,1)S(1)}, u32[]{:S(2)}, u32[]{:S(2)}) collective-permute-start(bf16[2,264,256]{2,1,0:T(8,128)(2,1)S(1)} %convolution_convert_fusion), channel_id=1, source_target_pairs={{0,15},{8,7},{16,31},{24,23},{32,47},{40,39},{48,63},{56,55},{64,7... | collective-permute-start | bytes 811016 | tf_op jit(solution)/shard_map/ppermute | solution.py:22
  38.1 1.3 %collective-permute-start.2 = (bf16[2,264,256]{2,1,0:T(8,128)(2,1)S(1)}, bf16[2,264,256]{2,1,0:T(8,128)(2,1)S(1)}, u32[]{:S(2)}, u32[]{:S(2)}) collective-permute-start(bf16[2,264,256]{2,1,0:T(8,128)(2,1)S(1)} %convolution_convert_fusion.1), channel_id=1, source_target_pairs={{0,1},{8,9},{16,17},{24,25},{32,33},{40,41},{48,49},{56,57},{64,65... | collective-permute-start | bytes 811016 | tf_op jit(solution)/shard_map/ppermute | solution.py:22
  39.5 0.3 fusion.8.refs_0_
  39.8 0.0 collective-permute-done.1.refs_2_
  39.8 22.7 %collective-permute-done.refs_1_ = bf16[2,264,256]{2,1,0:T(8,128)(2,1)S(1)} collective-permute-done((bf16[2,264,256]{2,1,0:T(8,128)(2,1)S(1)}, bf16[2,264,256]{2,1,0:T(8,128)(2,1)S(1)}, u32[]{:S(2)}, u32[]{:S(2)}) %collective-permute-start) | collective-permute-done | bytes 270368 | tf_op jit(solution)/shard_map/ppermute | solution.py:22
  62.5 4.7 %weights.1.refs_5_ = bf16[2,256,256]{2,1,0:T(8,128)(2,1)S(1)} custom-call(f32[2,264,256]{2,1,0:T(8,128)S(1)} %fusion.8.refs_0_, bf16[2,264,256]{2,1,0:T(8,128)(2,1)S(1)} %collective-permute-done.refs_1_, bf16[2,264,256]{2,1,0:T(8,128)(2,1)S(1)} %collective-permute-done.1.refs_2_), custom_call_target="tpu_custom_call" | custom-call | tf_op jit(solution)/shard_map/weights/pallas_call | solution.py:91
  67.2 0.0 collective-permute-done.3.refs_4_
  67.2 0.0 collective-permute-done.2.refs_3_
  67.2 0.0 all-to-all-done
  67.3 0.3 convert_reduce_fusion
  67.5 0.3 convert_bitcast_fusion
  67.8 0.2 copy.14
  68.0 0.6 add_convert_fusion
  68.6 0.7 copy.17
  69.3 43.9 %all_to_all.23 = bf16[2,256,8,128]{3,2,0,1:T(8,128)(2,1)S(1)} all-to-all(bf16[2,256,8,128]{3,2,0,1:T(8,128)(2,1)S(1)} %copy.17), channel_id=1, replica_groups=mesh['mem'=64,'patch'=16] {'mem'}, dimensions={1} | all-to-all | bytes 2097152 | tf_op jit(solution)/shard_map/all_to_all | solution.py:133
  113.2 1.2 %copy.29 = bf16[2,4,8,64,128]{4,2,3,1,0:T(8,128)(2,1)} copy(bf16[2,4,8,64,128]{4,2,0,1,3:T(8,128)(2,1)S(1)} %bitcast.22) | data formatting | bytes 2097152 | tf_op jit(solution)/shard_map/all_to_all | solution.py:133
  (4 shorter events, 0.1 us)
Async XLA Ops:
  0.0 1.2 %copy-start = (bf16[2,4,8,8192]{3,2,1,0:T(8,128)(2,1)S(1)}, bf16[2,4,8,8192]{3,2,1,0:T(8,128)(2,1)}, u32[]{:S(2)}) copy-start(bf16[2,4,8,8192]{3,2,1,0:T(8,128)(2,1)} %param.5) | copy-start | bytes 3145732
  0.0 20.7 %copy-start.1 = (bf16[2,512]{1,0:T(2,128)(2,1)S(1)}, bf16[2,512]{1,0:T(2,128)(2,1)}, u32[]{:S(2)}) copy-start(bf16[2,512]{1,0:T(2,128)(2,1)} %param.9) | copy-start | bytes 6148
  0.0 20.7 %copy-start.2 = (bf16[2,512]{1,0:T(2,128)(2,1)S(1)}, bf16[2,512]{1,0:T(2,128)(2,1)}, u32[]{:S(2)}) copy-start(bf16[2,512]{1,0:T(2,128)(2,1)} %param.8) | copy-start | bytes 6148
  0.0 20.8 %copy-start.4 = (bf16[2,256,512]{2,1,0:T(8,128)(2,1)S(1)}, bf16[2,256,512]{2,1,0:T(8,128)(2,1)}, u32[]{:S(2)}) copy-start(bf16[2,256,512]{2,1,0:T(8,128)(2,1)} %param.6) | copy-start | bytes 1572868
  1.2 19.5 %copy-start.3 = (bf16[2,512]{1,0:T(2,128)(2,1)S(1)}, bf16[2,512]{1,0:T(2,128)(2,1)}, u32[]{:S(2)}) copy-start(bf16[2,512]{1,0:T(2,128)(2,1)} %param.7) | copy-start | bytes 6148
  2.5 64.8 %all-to-all-start = ((bf16[64,2,4,8,128]{4,3,2,1,0:T(8,128)(2,1)}), bf16[64,2,4,8,128]{4,3,2,1,0:T(8,128)(2,1)S(1)}, u32[]{:S(2)}, u32[]{:S(2)}) async-start(bf16[64,2,4,8,128]{4,3,2,1,0:T(8,128)(2,1)} %bitcast_bitcast_fusion), calls=%async_computation | async-start | bytes 2097152 | tf_op jit(solution)/shard_map/all_to_all | solution.py:121
  21.2 18.7 %collective-permute-start.1 = (bf16[2,264,256]{2,1,0:T(8,128)(2,1)S(1)}, bf16[2,264,256]{2,1,0:T(8,128)(2,1)S(1)}, u32[]{:S(2)}, u32[]{:S(2)}) collective-permute-start(bf16[2,264,256]{2,1,0:T(8,128)(2,1)S(1)} %convolution_convert_fusion), channel_id=1, source_target_pairs={{1,0},{2,1},{3,2},{4,3},{5,4},{6,5},{7,6},{9,8},{10,9},{11,10},{12... | collective-permute-start | bytes 811016 | tf_op jit(solution)/shard_map/ppermute | solution.py:22
  22.8 39.7 %collective-permute-start = (bf16[2,264,256]{2,1,0:T(8,128)(2,1)S(1)}, bf16[2,264,256]{2,1,0:T(8,128)(2,1)S(1)}, u32[]{:S(2)}, u32[]{:S(2)}) collective-permute-start(bf16[2,264,256]{2,1,0:T(8,128)(2,1)S(1)} %convolution_convert_fusion.1), channel_id=1, source_target_pairs={{1,2},{2,3},{3,4},{4,5},{5,6},{6,7},{7,8},{9,10},{10,11},{11,12},{... | collective-permute-start | bytes 811016 | tf_op jit(solution)/shard_map/ppermute | solution.py:22
  24.1 43.1 %collective-permute-start.3 = (bf16[2,264,256]{2,1,0:T(8,128)(2,1)S(1)}, bf16[2,264,256]{2,1,0:T(8,128)(2,1)S(1)}, u32[]{:S(2)}, u32[]{:S(2)}) collective-permute-start(bf16[2,264,256]{2,1,0:T(8,128)(2,1)S(1)} %convolution_convert_fusion), channel_id=1, source_target_pairs={{0,15},{8,7},{16,31},{24,23},{32,47},{40,39},{48,63},{56,55},{64,7... | collective-permute-start | bytes 811016 | tf_op jit(solution)/shard_map/ppermute | solution.py:22
  38.1 29.0 %collective-permute-start.2 = (bf16[2,264,256]{2,1,0:T(8,128)(2,1)S(1)}, bf16[2,264,256]{2,1,0:T(8,128)(2,1)S(1)}, u32[]{:S(2)}, u32[]{:S(2)}) collective-permute-start(bf16[2,264,256]{2,1,0:T(8,128)(2,1)S(1)} %convolution_convert_fusion.1), channel_id=1, source_target_pairs={{0,1},{8,9},{16,17},{24,25},{32,33},{40,41},{48,49},{56,57},{64,65... | collective-permute-start | bytes 811016 | tf_op jit(solution)/shard_map/ppermute | solution.py:22
